TPU v7x, 128 devices: a whole 4x4x4 slice. The times are simulated.
128 devices in a mesh: rows: 8 (over z, core), model: 16 (over y, x).
Axes of the slice: x: 4, y: 4, z: 4, core: 2. Of those that a mesh axis runs over, the one named last changes fastest.
Arguments:
- train_query: bfloat16 [8192, 8192], P('rows', 'model'), may hold values from -0.0625 to 0.0625
- low_query: bfloat16 [8192, 16], P('rows'), may hold values from -0.0625 to 0.0625
- high_query: bfloat16 [16, 8192], P(None, 'model'), may hold values from -1.5 to 1.5
- train_key: bfloat16 [8192, 1024], P('rows', 'model'), may hold values from -0.0625 to 0.0625
- low_key: bfloat16 [8192, 16], P('rows'), may hold values from -0.0625 to 0.0625
- high_key: bfloat16 [16, 1024], P(None, 'model'), may hold values from -1.5 to 1.5
- train_value: bfloat16 [8192, 1024], P('rows', 'model'), may hold values from -0.0625 to 0.0625
- low_value: bfloat16 [8192, 16], P('rows'), may hold values from -0.0625 to 0.0625
- high_value: bfloat16 [16, 1024], P(None, 'model'), may hold values from -1.5 to 1.5
- train_mixed: bfloat16 [8192, 8192], P('model', 'rows'), may hold values from -0.0625 to 0.0625
- low_mixed: bfloat16 [8192, 16], P('model'), may hold values from -0.0625 to 0.0625
- high_mixed: bfloat16 [16, 8192], P(None, 'rows'), may hold values from -1.5 to 1.5
- norm_train: float32 [8192], P(('rows', 'model')), may hold values from 0.25 to 1.75
- norm_step: float32 [8192], P(('rows', 'model')), may hold values from -0.3 to 0.3
Outputs:
- serving_query: bfloat16 [8192, 8192], P('model')
- serving_key: bfloat16 [1024, 8192], P('model')
- serving_value: bfloat16 [1024, 8192], P('model')
- serving_mixed: bfloat16 [8192, 8192], P(None, 'model')
- serve_norm: bfloat16 [8192], replicated
All inputs are finite; a program needn't handle non-finite values.
Results may differ from a plain program's by a relative error of at most 0.001.
Values may be sent and summed in bfloat16 or wider, within the bound.
A program may use at most 128 MiB of HBM per device.

v0:
```python
import jax
import jax.numpy as jnp
from jax import lax
from jax.sharding import Mesh
from jax.sharding import PartitionSpec as P

ROWS = ("rows_0", "rows_1")
ROWS_MODEL = ("rows_0", "rows_1", "model_0", "model_1")
MODEL = ("model_0", "model_1")


mix_rate = 0.5


def turned_gather(arrays, axis, dims):
    turned = [jnp.moveaxis(a, dim, 0) for a, dim in zip(arrays, dims)]
    widths = [t[0].size for t in turned]
    both = jnp.concatenate([t.reshape(-1, w) for t, w in zip(turned, widths)], axis=1)
    out = lax.all_gather(both, axis, axis=0, tiled=True)
    parts = jnp.split(out, [sum(widths[:k]) for k in range(1, len(widths))], axis=1)
    return tuple(
        (
            jnp.moveaxis(b.reshape(-1, *t.shape[1:]), 0, dim)
            for b, t, dim in zip(parts, turned, dims)
        )
    )


def in_order(parts, dim):
    parts = jnp.moveaxis(parts, 0, dim)
    shape = parts.shape
    return parts.reshape(*shape[:dim], shape[dim] * shape[dim + 1], *shape[dim + 2 :])


def stacked_from(array, axes, order):
    parts = array
    for k in order:
        parts = lax.all_gather(parts, axes[k])
    done = order[::-1]
    back = [done.index(k) for k in range(len(axes))]
    parts = parts.transpose(*back, *range(len(axes), parts.ndim))
    return parts.reshape(-1, *array.shape)


def whole_of(array, axes, order, dim):
    return in_order(stacked_from(array, axes, order), dim)


def body(
    train_query,
    low_query,
    high_query,
    train_key,
    low_key,
    high_key,
    train_value,
    low_value,
    high_value,
    train_mixed,
    low_mixed,
    high_mixed,
    norm_train,
    norm_step,
):
    whole_query = train_query.astype(jnp.float32) + mix_rate * jnp.dot(
        low_query, high_query, preferred_element_type=jnp.float32
    )
    whole_key = train_key.astype(jnp.float32) + mix_rate * jnp.dot(
        low_key, high_key, preferred_element_type=jnp.float32
    )
    whole_value = train_value.astype(jnp.float32) + mix_rate * jnp.dot(
        low_value, high_value, preferred_element_type=jnp.float32
    )
    whole_mixed = train_mixed.astype(jnp.float32) + mix_rate * jnp.dot(
        low_mixed, high_mixed, preferred_element_type=jnp.float32
    )
    narrow_query, narrow_key, narrow_value, narrow_mixed = (
        whole_query.astype(jnp.bfloat16),
        whole_key.astype(jnp.bfloat16),
        whole_value.astype(jnp.bfloat16),
        whole_mixed.astype(jnp.bfloat16),
    )
    serving_query, serving_key, serving_value, serving_mixed = turned_gather(
        (narrow_query, narrow_key, narrow_value, narrow_mixed), ROWS, (0, 0, 0, 1)
    )
    serving_query, serving_key, serving_value, serving_mixed = (
        serving_query.T,
        serving_key.T,
        serving_value.T,
        serving_mixed.T,
    )
    serve_norm = whole_of(
        (norm_train + norm_step).astype(jnp.bfloat16), ROWS_MODEL, (0, 2, 3, 1), 0
    )
    return (serving_query, serving_key, serving_value, serving_mixed, serve_norm)


def solution(mesh):
    finer = Mesh(mesh.devices.reshape(4, 2, 4, 4), ("rows_0", "rows_1", "model_0", "model_1"))
    return jax.shard_map(
        body,
        mesh=finer,
        in_specs=(
            P(ROWS, MODEL),
            P(ROWS, None),
            P(None, MODEL),
            P(ROWS, MODEL),
            P(ROWS, None),
            P(None, MODEL),
            P(ROWS, MODEL),
            P(ROWS, None),
            P(None, MODEL),
            P(MODEL, ROWS),
            P(MODEL, None),
            P(None, ROWS),
            P(ROWS_MODEL),
            P(ROWS_MODEL),
        ),
        out_specs=(P(MODEL, None), P(MODEL, None), P(MODEL, None), P(None, MODEL), P()),
        check_vma=False,
    )
```

profile of v0, /device:TPU:1, one launch (start us, length us, event | category | flops | bytes accessed | tf_op | source)
XLA Modules:
  0.0 144.0 jit_solution(17631566383366275951)
XLA Ops:
  7.2 0.0 copy-start
  7.3 0.0 all-gather.7.cloned.1.call-start
  7.3 1.6 %copy.35 = bf16[1024,512]{0,1:T(8,128)(2,1)S(1)} copy(bf16[1024,512]{1,0:T(8,128)(2,1)} %param.14) | data formatting | bytes 2097152 | tf_op args[0]
  8.9 1.2 fusion
  10.1 0.2 fusion.4
  10.4 0.0 copy-done.6
  10.4 0.0 copy-done.9
  10.4 0.2 fusion.3
  10.6 0.5 add_convert_fusion.1
  11.1 1.6 %pad_maximum_fusion = bf16[1024,1152]{0,1:T(8,128)(2,1)} fusion(bf16[1024,512]{0,1:T(8,128)(2,1)S(1)} %fusion, bf16[1024,64]{0,1:T(8,128)(2,1)S(1)} %fusion.4, bf16[1024,64]{0,1:T(8,128)(2,1)S(1)} %fusion.3, bf16[1024,512]{0,1:T(8,128)(2,1)S(1)} %add_convert_fusion.1), kind=kLoop, calls=%fused_computation.1 | loop fusion | flops 9437184 | bytes 4718592 | tf_op jit(solution)/shard_map/concatenate | solution.py:18
  12.7 0.0 all-gather.7.cloned.1.call-update
  12.8 0.6 copy-done.12
  13.4 0.6 dynamic-slice
  14.7 0.2 dynamic-update-slice
  14.9 10.5 %all-reduce = bf16[256]{0:T(256)(128)(2,1)S(1)} all-reduce(bf16[256]{0:T(256)(128)(2,1)S(1)} %dynamic-update-slice), channel_id=2, replica_groups=mesh['rows_0'=4,'rows_1'=2,'model_0'=4,'model_1'=4] {'rows_0'}, use_global_device_ids=true, to_apply=%add | all-reduce | flops 256 | bytes 1024
  25.5 0.1 reshape.17
  25.5 8.4 %all-gather.4 = bf16[4,4,64]{2,1,0:T(4,128)(2,1)S(1)} all-gather(bf16[1,4,64]{2,1,0:T(4,128)(2,1)S(1)} %reshape.17), channel_id=3, replica_groups=mesh['rows_0'=4,'rows_1'=2,'model_0'=4,'model_1'=4] {'model_0'}, dimensions={0}, use_global_device_ids=true | all-gather | bytes 2560 | tf_op jit(solution)/shard_map/all_gather | solution.py:38
  33.9 10.4 %all-gather.2 = bf16[16,4,64]{2,1,0:T(4,128)(2,1)S(1)} all-gather(bf16[4,4,64]{2,1,0:T(4,128)(2,1)S(1)} %all-gather.4), channel_id=4, replica_groups=mesh['rows_0'=4,'rows_1'=2,'model_0'=4,'model_1'=4] {'model_1'}, dimensions={0}, use_global_device_ids=true | all-gather | bytes 10240 | tf_op jit(solution)/shard_map/all_gather | solution.py:38
  44.3 7.7 %all-gather.3 = bf16[8,4,4,64]{3,1,0,2:T(4,128)(2,1)S(1)} all-gather(bf16[4,4,4,64]{3,1,0,2:T(4,128)(2,1)S(1)} %bitcast.22), channel_id=5, replica_groups=mesh['rows_0'=4,'rows_1'=2,'model_0'=4,'model_1'=4] {'rows_1'}, dimensions={0}, use_global_device_ids=true | all-gather | bytes 24576 | tf_op jit(solution)/shard_map/all_gather | solution.py:38
  52.1 0.7 reshape_reshape.3
  52.8 57.7 %all-gather.7.cloned.1.call-done = bf16[8192,1152]{0,1:T(8,128)(2,1)} async-done(((bf16[1024,1152]{0,1:T(8,128)(2,1)}), bf16[8192,1152]{0,1:T(8,128)(2,1)}) %all-gather.7.cloned.1.call-update) | async-done | bytes 18874384 | tf_op jit(solution)/shard_map/all_gather | solution.py:19
  110.5 11.7 %fusion.5 = (bf16[8192,512]{0,1:T(8,128)(2,1)}, bf16[512,8192]{1,0:T(8,128)(2,1)}) fusion(bf16[8192,1152]{0,1:T(8,128)(2,1)} %all-gather.7.cloned.1.call-done), kind=kLoop, calls=%fused_computation.14 | loop fusion | bytes 33554432 | tf_op jit(solution)/shard_map/split | solution.py:20
  122.1 11.9 %copy.39 = bf16[8192,512]{1,0:T(8,128)(2,1)} copy(bf16[8192,512]{0,1:T(8,128)(2,1)} %get-tuple-element.35) | data formatting | bytes 16777216
  134.1 3.0 %slice_bitcast_fusion.1 = (bf16[64,8192]{1,0:T(8,128)(2,1)}, bf16[64,8192]{1,0:T(8,128)(2,1)}) fusion(bf16[8192,1152]{0,1:T(8,128)(2,1)} %all-gather.7.cloned.1.call-done), kind=kLoop, calls=%fused_computation.11 | loop fusion | bytes 4194304 | tf_op jit(solution)/shard_map/transpose | solution.py:89
  (27 shorter events, 0.1 us)
Async XLA Ops:
  7.2 1.7 %copy-start = (bf16[16,1024]{1,0:T(8,128)(2,1)S(1)}, bf16[16,1024]{1,0:T(8,128)(2,1)}, u32[]{:S(2)}) copy-start(bf16[16,1024]{1,0:T(8,128)(2,1)} %param.25) | copy-start | bytes 98308
  7.2 1.7 %copy-start.1 = (bf16[512,1024]{1,0:T(8,128)(2,1)S(1)}, bf16[512,1024]{1,0:T(8,128)(2,1)}, u32[]{:S(2)}) copy-start(bf16[512,1024]{1,0:T(8,128)(2,1)} %param.23) | copy-start | bytes 3145732
  7.2 2.9 %copy-start.5 = (bf16[1024,16]{0,1:T(8,128)(2,1)S(1)}, bf16[1024,16]{0,1:T(8,128)(2,1)}, u32[]{:S(2)}) copy-start(bf16[1024,16]{0,1:T(8,128)(2,1)} %param.21) | copy-start | bytes 98308
  7.2 2.9 %copy-start.8 = (bf16[16,64]{1,0:T(8,128)(2,1)S(1)}, bf16[16,64]{1,0:T(8,128)(2,1)}, u32[]{:S(2)}) copy-start(bf16[16,64]{1,0:T(8,128)(2,1)} %param.22) | copy-start | bytes 6148
  7.2 2.9 %copy-start.2 = (bf16[1024,64]{0,1:T(8,128)(2,1)S(1)}, bf16[1024,64]{0,1:T(8,128)(2,1)}, u32[]{:S(2)}) copy-start(bf16[1024,64]{0,1:T(8,128)(2,1)} %param.20) | copy-start | bytes 393220
  7.2 3.1 %copy-start.6 = (bf16[1024,16]{0,1:T(8,128)(2,1)S(1)}, bf16[1024,16]{0,1:T(8,128)(2,1)}, u32[]{:S(2)}) copy-start(bf16[1024,16]{0,1:T(8,128)(2,1)} %param.18) | copy-start | bytes 98308
  7.2 3.1 %copy-start.9 = (bf16[16,64]{1,0:T(8,128)(2,1)S(1)}, bf16[16,64]{1,0:T(8,128)(2,1)}, u32[]{:S(2)}) copy-start(bf16[16,64]{1,0:T(8,128)(2,1)} %param.19) | copy-start | bytes 6148
  7.2 3.1 %copy-start.3 = (bf16[1024,64]{0,1:T(8,128)(2,1)S(1)}, bf16[1024,64]{0,1:T(8,128)(2,1)}, u32[]{:S(2)}) copy-start(bf16[1024,64]{0,1:T(8,128)(2,1)} %param.17) | copy-start | bytes 393220
  7.3 3.4 %copy-start.4 = (bf16[1024,16]{0,1:T(8,128)(2,1)S(1)}, bf16[1024,16]{0,1:T(8,128)(2,1)}, u32[]{:S(2)}) copy-start(bf16[1024,16]{0,1:T(8,128)(2,1)} %param.15) | copy-start | bytes 98308
  7.3 3.4 %copy-start.7 = (bf16[16,512]{1,0:T(8,128)(2,1)S(1)}, bf16[16,512]{1,0:T(8,128)(2,1)}, u32[]{:S(2)}) copy-start(bf16[16,512]{1,0:T(8,128)(2,1)} %param.16) | copy-start | bytes 49156
  7.3 103.2 %all-gather.7.cloned.1.call-start = ((), (), s32[]{:S(2)}) async-start(), calls=%async_computation | async-start | bytes 21233664 | tf_op jit(solution)/shard_map/all_gather | solution.py:19
  12.7 0.7 copy-start.12
  12.7 1.9 %copy-start.10 = (f32[64]{0:T(128)S(1)}, f32[64]{0:T(128)}, u32[]{:S(2)}) copy-start(f32[64]{0:T(128)} %param.26) | copy-start | bytes 772
  12.7 1.9 %copy-start.11 = (f32[64]{0:T(128)S(1)}, f32[64]{0:T(128)}, u32[]{:S(2)}) copy-start(f32[64]{0:T(128)} %param.27) | copy-start | bytes 772
Sparse Core Ops, SparseCore 0:
  12.9 97.5 all-gather.6
where the time goes:
time: 145 us; the launch traced here: 144 us
  waiting for transfers between devices  57.7 us (40%)
  blocking collectives  37 us (26%)
  local copies, waits for them, and re-layouts  30.5 us (21%)
  between operations  14.9 us (10%)
  matrix products  2.1 us (1%)
  other arithmetic  1.62 us (1%)
    all_gather x1, waiting for transfers between devices, turned_gather(): out = lax.all_gather(both, axis, axis=0, tiled=True)  57.7 us
    all_gather x3, blocking collectives, stacked_from(): parts = lax.all_gather(parts, axes[k])  26.5 us
    unnamed x32, local copies, waits for them, and re-layouts  15.1 us
    split x1, local copies, waits for them, and re-layouts, turned_gather(): jnp.split(out, [sum(widths[:k]) for k in range(1, len(widths))], axis=1)  11.7 us
    unnamed x1, blocking collectives  10.5 us
    transpose x1, local copies, waits for them, and re-layouts, body(): serving_query, serving_key, serving_value, serving_mixed = (serving_query...  3.04 us
  transfers between devices with their start and end apart: 1, of which 1 were waited for; matrix products, arithmetic and copies ran while one was open for 1% of the time, Pallas kernels for 0%

commit v1 on v0

v1 whole, which is shorter than its diff:
```python
import jax
import jax.numpy as jnp
from jax import lax
from jax.experimental import pallas as pl
from jax.experimental.pallas import tpu as pltpu
from jax.sharding import PartitionSpec as P

MESH = pl.DeviceIdType.MESH
HBM = pl.BlockSpec(memory_space=pltpu.HBM)
VMEM = pl.BlockSpec(memory_space=pltpu.VMEM)

mix_rate = 0.5

PIECES = 18
HALF = PIECES // 2


def comm_kernel(
    tq, tk, tv, tm, lq, hq, lk, hk, lv, hv, lm, hm, na, nb,
    b, nz,
    xq, xkv, xm, slq, shq, slk, shk, slv, shv, slm, shm, sna, snb, nx, ny,
    ld, send, near_a, near_b, far_a, far_b, part_send, part_recv,
    nx_send, nx_recv, ny_send, ny_recv, nz_send, nz_recv, np_send, np_recv,
):
    rows = lax.axis_index("rows")
    model = lax.axis_index("model")
    z, core = rows // 2, rows % 2
    y, x = model // 4, model % 4
    up, down = (z + 1) % 4, (z + 3) % 4
    far = (z + 2) % 4
    to_up = {"rows": up * 2 + core}
    to_down = {"rows": down * 2 + core}
    to_part = {"rows": z * 2 + 1 - core}
    to_x = [{"model": y * 4 + (x + d) % 4} for d in (1, 2, 3)]
    to_y = [{"model": ((y + d) % 4) * 4 + x} for d in (1, 2, 3)]

    loads = [
        (tk, xkv.at[pl.ds(0, 64)]), (tv, xkv.at[pl.ds(64, 64)]),
        (lk, slk), (hk, shk), (lv, slv), (hv, shv),
        (na, sna), (nb, snb),
        (lq, slq), (hq, shq), (tq, xq),
        (lm, slm), (hm, shm), (tm, xm),
    ]
    loads = [pltpu.make_async_copy(s, d, ld.at[i]) for i, (s, d) in enumerate(loads)]
    for c in loads:
        c.start()
    barrier = pltpu.get_barrier_semaphore()
    for peer in [to_up, to_down, to_part] + to_x + to_y:
        pl.semaphore_signal(barrier, inc=1, device_id=peer, device_id_type=MESH)

    def low_rank(high, low):
        return mix_rate * lax.dot_general(
            high, low, (((0,), (0,)), ((), ())), preferred_element_type=jnp.float32
        )

    for c in loads[:8]:
        c.wait()
    for j in range(2):
        cols = pl.ds(j * 512, 512)
        for k, (high, low) in enumerate(((shk, slk), (shv, slv))):
            half = pl.ds(k * 64, 64)
            b[rows, j, half, :] = (
                xkv[half, cols].astype(jnp.float32) + low_rank(high[...], low[:, cols])
            ).astype(jnp.bfloat16)
    gain = sna[...] + snb[...]
    nx[x] = jnp.concatenate([gain, gain], axis=1)

    def copy_to(src, index, send_sem, recv_sem, to):
        return pltpu.make_async_remote_copy(
            src_ref=b.at[src, index], dst_ref=b.at[src, index], send_sem=send_sem,
            recv_sem=recv_sem, device_id=to, device_id_type=MESH,
        )

    def send_own(k):
        copy_to(rows, k, send.at[0], near_a.at[k], to_up).start()
        copy_to(rows, k, send.at[1], near_b.at[k], to_down).start()

    def to_partner(chip, k):
        copy_to(chip * 2 + core, k, part_send.at[chip], part_recv.at[chip], to_part).start()

    pl.semaphore_wait(barrier, 9)
    send_own(0)
    send_own(1)

    nx_copies = [
        pltpu.make_async_remote_copy(
            src_ref=nx.at[x], dst_ref=nx.at[x], send_sem=nx_send.at[d], recv_sem=nx_recv.at[d],
            device_id=to, device_id_type=MESH,
        )
        for d, to in enumerate(to_x)
    ]
    for c in nx_copies:
        c.start()
    to_partner(z, 0)
    to_partner(z, 1)

    for c in loads[8:]:
        c.wait()

    def make_query(i):
        left, top = (i // 4) * 512, (i % 4) * 128
        left, top = pl.multiple_of(left, 512), pl.multiple_of(top, 128)
        part = low_rank(shq[:, pl.ds(top, 128)], slq[:, pl.ds(left, 512)])
        base = xq[pl.ds(left, 512), pl.ds(top, 128)].astype(jnp.float32)
        b[rows, 2 + i] = (base.T + part).astype(jnp.bfloat16)

    def make_mixed(i):
        top = pl.multiple_of(i * 128, 128)
        part = low_rank(shm[:, pl.ds(top, 128)], slm[...])
        base = xm[:, pl.ds(top, 128)].astype(jnp.float32)
        b[rows, 10 + i] = (base.T + part).astype(jnp.bfloat16)

    make_query(0)

    @pl.loop(1, 8)
    def _(i):
        make_query(i)
        send_own(1 + i)
        to_partner(z, 1 + i)

    make_mixed(0)
    send_own(9)
    to_partner(z, 9)

    @pl.loop(1, 8)
    def _(i):
        make_mixed(i)
        send_own(9 + i)
        to_partner(z, 9 + i)

    for c in nx_copies:
        c.wait()
    lane = lax.broadcasted_iota(jnp.int32, (1, 128), 1)
    ny[y, 0:1] = jnp.where(lane < 64, nx[0], nx[1])
    ny[y, 1:2] = jnp.where(lane < 64, nx[2], nx[3])
    send_own(17)
    to_partner(z, 17)
    ny_copies = [
        pltpu.make_async_remote_copy(
            src_ref=ny.at[y], dst_ref=ny.at[y], send_sem=ny_send.at[d], recv_sem=ny_recv.at[d],
            device_id=to, device_id_type=MESH,
        )
        for d, to in enumerate(to_y)
    ]
    for c in ny_copies:
        c.start()

    def near(first, last):
        @pl.loop(first, last)
        def _(j):
            a = 2 * j
            copy_to(down * 2 + core, a, send.at[0], near_a.at[a], to_up).wait_recv()
            copy_to(down * 2 + core, a, send.at[2], far_a.at[j], to_up).start()
            to_partner(down, a)
            copy_to(up * 2 + core, a, send.at[1], near_b.at[a], to_down).wait_recv()
            to_partner(up, a)
            c = 2 * j + 1
            copy_to(down * 2 + core, c, send.at[0], near_a.at[c], to_up).wait_recv()
            to_partner(down, c)
            copy_to(up * 2 + core, c, send.at[1], near_b.at[c], to_down).wait_recv()
            copy_to(up * 2 + core, c, send.at[3], far_b.at[j], to_down).start()
            to_partner(up, c)

    def nz_copy(src, send_sem, recv_sem, to):
        return pltpu.make_async_remote_copy(
            src_ref=nz.at[src], dst_ref=nz.at[src], send_sem=send_sem, recv_sem=recv_sem,
            device_id=to, device_id_type=MESH,
        )

    near(0, 2)
    for c in ny_copies:
        c.wait()
    for i in range(4):
        nz[rows, 2 * i : 2 * i + 2] = ny[i]
    near(2, 4)
    n_up = nz_copy(rows, nz_send.at[0], nz_recv.at[0], to_up)
    n_down = nz_copy(rows, nz_send.at[1], nz_recv.at[1], to_down)
    n_up.start()
    n_down.start()
    near(4, 6)
    n_up.wait()
    n_down.wait()
    n_far = nz_copy(down * 2 + core, nz_send.at[2], nz_recv.at[2], to_up)
    n_far.start()
    near(6, 8)
    n_far.wait()
    n_part = [nz_copy(c * 2 + core, np_send.at[c], np_recv.at[c], to_part) for c in range(4)]
    for c in n_part:
        c.start()
    near(8, 9)

    @pl.loop(0, HALF)
    def _(j):
        copy_to(far * 2 + core, 2 * j, send.at[2], far_a.at[j], to_up).wait_recv()
        to_partner(far, 2 * j)
        copy_to(far * 2 + core, 2 * j + 1, send.at[3], far_b.at[j], to_down).wait_recv()
        to_partner(far, 2 * j + 1)

    for c in n_part:
        c.wait()

    def all_of(src, count, send_sem, recv_sem, to):
        part = b.at[src, pl.ds(0, count)]
        return pltpu.make_async_remote_copy(
            src_ref=part, dst_ref=part, send_sem=send_sem, recv_sem=recv_sem,
            device_id=to, device_id_type=MESH,
        )

    all_of(rows, PIECES, send.at[0], near_a.at[0], to_up).wait_send()
    all_of(rows, PIECES, send.at[1], near_b.at[0], to_down).wait_send()
    all_of(rows, HALF, send.at[2], far_a.at[0], to_up).wait_send()
    all_of(rows, HALF, send.at[3], far_b.at[0], to_down).wait_send()
    for c in range(4):
        all_of(c * 2 + core, PIECES, part_send.at[c], part_recv.at[c], to_part).wait_send()
        all_of(c * 2 + 1 - core, PIECES, part_send.at[c], part_recv.at[c], to_part).wait_recv()


def comm(*args):
    bf16, f32 = jnp.bfloat16, jnp.float32
    dma = pltpu.SemaphoreType.DMA
    return pl.pallas_call(
        comm_kernel,
        out_shape=[pltpu.VMEM((8, PIECES, 128, 512), bf16), pltpu.VMEM((8, 8, 128), f32)],
        in_specs=[HBM] * len(args),
        out_specs=[VMEM] * 2,
        scratch_shapes=[
            pltpu.VMEM((1024, 512), bf16), pltpu.VMEM((128, 1024), bf16), pltpu.VMEM((512, 1024), bf16),
            pltpu.VMEM((16, 1024), bf16), pltpu.VMEM((16, 512), bf16),
            pltpu.VMEM((16, 1024), bf16), pltpu.VMEM((16, 64), bf16),
            pltpu.VMEM((16, 1024), bf16), pltpu.VMEM((16, 64), bf16),
            pltpu.VMEM((16, 512), bf16), pltpu.VMEM((16, 1024), bf16),
            pltpu.VMEM((1, 64), f32), pltpu.VMEM((1, 64), f32),
            pltpu.VMEM((4, 1, 128), f32), pltpu.VMEM((4, 2, 128), f32),
            dma((14,)), dma((4,)), dma((PIECES,)), dma((PIECES,)), dma((HALF,)), dma((HALF,)),
            dma((4,)), dma((4,)),
            dma((3,)), dma((3,)), dma((3,)), dma((3,)), dma((3,)), dma((3,)), dma((4,)), dma((4,)),
        ],
        compiler_params=pltpu.CompilerParams(
            collective_id=0, has_side_effects=True, vmem_limit_bytes=44 * 2**20
        ),
        name="comm",
    )(*args)


def write_kernel(b, nz, q, k, v, m, n, sem):
    for r in range(8):
        for j in range(2):
            cols = pl.ds(r * 1024 + j * 512, 512)
            pltpu.make_async_copy(b.at[r, j, pl.ds(0, 64)], k.at[:, cols], sem.at[0]).start()
            pltpu.make_async_copy(b.at[r, j, pl.ds(64, 64)], v.at[:, cols], sem.at[1]).start()

    @pl.loop(0, 8)
    def _(r):
        for i in range(8):
            pltpu.make_async_copy(
                b.at[r, 2 + i],
                q.at[pl.ds(i % 4 * 128, 128), pl.ds(pl.multiple_of(r * 1024 + i // 4 * 512, 512), 512)],
                sem.at[2],
            ).start()
            pltpu.make_async_copy(
                b.at[r, 10 + i], m.at[pl.ds(pl.multiple_of(r * 1024 + i * 128, 128), 128)], sem.at[3]
            ).start()

    n[...] = nz[...].reshape(64, 128).astype(jnp.bfloat16)
    for i, ref in enumerate((k, v, q, m)):
        pltpu.make_async_copy(ref, ref, sem.at[i]).wait()


def write(b, nz):
    bf16 = jnp.bfloat16
    shapes = [(512, 8192), (64, 8192), (64, 8192), (8192, 512), (64, 128)]
    return pl.pallas_call(
        write_kernel,
        out_shape=[jax.ShapeDtypeStruct(s, bf16) for s in shapes],
        in_specs=[VMEM] * 2,
        out_specs=[HBM] * 4 + [VMEM],
        scratch_shapes=[pltpu.SemaphoreType.DMA((4,))],
        compiler_params=pltpu.CompilerParams(vmem_limit_bytes=4 * 2**20),
        name="write",
    )(b, nz)


def body(
    train_query, low_query, high_query, train_key, low_key, high_key, train_value, low_value, high_value,
    train_mixed, low_mixed, high_mixed, norm_train, norm_step,
):
    b, nz = comm(
        train_query, train_key.T, train_value.T, train_mixed,
        low_query.T, high_query, low_key.T, high_key, low_value.T, high_value, low_mixed.T, high_mixed,
        norm_train.reshape(1, 64), norm_step.reshape(1, 64),
    )
    q, k, v, m, n = write(b, nz)
    return q, k, v, m, n.reshape(8192)


def solution(mesh):
    R, M = "rows", "model"
    return jax.shard_map(
        body,
        mesh=mesh,
        in_specs=(
            P(R, M), P(R, None), P(None, M),
            P(R, M), P(R, None), P(None, M),
            P(R, M), P(R, None), P(None, M),
            P(M, R), P(M, None), P(None, R),
            P((R, M)), P((R, M)),
        ),
        out_specs=(P(M, None), P(M, None), P(M, None), P(None, M), P()),
        check_vma=False,
    )
```

time: 145 us -> 95.1 us (0.66)
  Pallas kernels: 0 us -> 94.3 us
  waiting for transfers between devices: 57.7 us -> 0 us
  blocking collectives: 37 us -> 0 us
  local copies, waits for them, and re-layouts: 30.5 us -> 0 us
  between operations: 14.9 us -> 0.65 us
  matrix products: 2.1 us -> 0 us
  other arithmetic: 1.62 us -> 0 us
    pallas_call x0 -> x2, Pallas kernels: none -> 94.3 us  [the longest x1 87.3 us: comm(): pl.pallas_call(comm_kernel, out_shape=[pltpu.VMEM((8, PIECES, 128, 512),...]
    all_gather x1 -> x0, waiting for transfers between devices: 57.7 us -> none  [turned_gather(): out = lax.all_gather(both, axis, axis=0, tiled=True)]
    all_gather x3 -> x0, blocking collectives: 26.5 us -> none  [stacked_from(): parts = lax.all_gather(parts, axes[k])]
    unnamed x32 -> x0, local copies, waits for them, and re-layouts: 15.1 us -> none
    split x1 -> x0, local copies, waits for them, and re-layouts: 11.7 us -> none  [turned_gather(): jnp.split(out, [sum(widths[:k]) for k in range(1, len(widths))], axis=1)]
    unnamed x1 -> x0, blocking collectives: 10.5 us -> none
    transpose x2 -> x0, local copies, waits for them, and re-layouts: 3.06 us -> none  [the longest x1 3.04 us: body(): serving_query, serving_key, serving_value, serving_mixed = (serving_query...]
    dot_general x4 -> x0, matrix products: 2.1 us -> none  [the longest x1 1.18 us: body(): jnp.dot(low_mixed, high_mixed, preferred_element_type=jnp.float32)]
  transfers between devices with their start and end apart: 1 -> 0, of which waited for: 1 -> 0; matrix products, arithmetic and copies ran while one was open for 1% -> 0% of each run, Pallas kernels for 0% -> 0%
where the time goes in v1:
time: 95.1 us; the launch traced here: 94.9 us
  Pallas kernels  94.3 us (99%)
    pallas_call x1, Pallas kernels, comm(): pl.pallas_call(comm_kernel, out_shape=[pltpu.VMEM((8, PIECES, 128, 512),...  87.3 us
    pallas_call x1, Pallas kernels, write(): pl.pallas_call(write_kernel, out_shape=[jax.ShapeDtypeStruct(s, bf16) for...  6.98 us

profile of v1, /device:TPU:1, one launch (start us, length us, event | category | flops | bytes accessed | tf_op | source)
XLA Modules:
  0.0 94.9 jit_solution(1055558901216503659)
XLA Ops:
  0.6 87.3 %comm.1 = (bf16[8,18,128,512]{3,2,1,0:T(8,128)(2,1)S(1)}, f32[8,8,128]{2,1,0:T(8,128)S(1)}) custom-call(bf16[1024,512]{1,0:T(8,128)(2,1)} %tq.1, bf16[64,1024]{1,0:T(8,128)(2,1)} %bitcast.9, bf16[64,1024]{1,0:T(8,128)(2,1)} %bitcast.10, bf16[512,1024]{1,0:T(8,128)(2,1)} %tm.1, bf16[16,1024]{1,0:T(8,128)(2,1)} %bitcast.11, bf16[16,512]{1,0:T(8,128)(2,1)} %hq.1, ...), custom_call_target="tpu_custom_call" | custom-call | tf_op jit(solution)/shard_map/comm/pallas_call | solution.py:221
  88.0 7.0 %write.1 = (bf16[512,8192]{1,0:T(8,128)(2,1)}, bf16[64,8192]{1,0:T(8,128)(2,1)}, bf16[64,8192]{1,0:T(8,128)(2,1)}, bf16[8192,512]{1,0:T(8,128)(2,1)}, bf16[64,128]{1,0:T(8,128)(2,1)}) custom-call(bf16[8,18,128,512]{3,2,1,0:T(8,128)(2,1)S(1)} %get-tuple-element.12.b, f32[8,8,128]{2,1,0:T(8,128)S(1)} %get-tuple-element.13.nz), custom_call_target="tpu_custom_call" | custom-call | tf_op jit(solution)/shard_map/write/pallas_call | solution.py:272

commit v2 on v1

v2 whole, which is shorter than its diff:
```python
import jax
import jax.numpy as jnp
from jax import lax
from jax.experimental import pallas as pl
from jax.experimental.pallas import tpu as pltpu
from jax.sharding import PartitionSpec as P

MESH = pl.DeviceIdType.MESH
HBM = pl.BlockSpec(memory_space=pltpu.HBM)
VMEM = pl.BlockSpec(memory_space=pltpu.VMEM)

mix_rate = 0.5

PIECES = 18
HALF = PIECES // 2


def comm_kernel(
    tq, tk, tv, tm, lq, hq, lk, hk, lv, hv, lm, hm, na, nb,
    b, nz,
    xq, xk, xv, xm, slq, shq, slk, shk, slv, shv, slm, shm, sna, snb, gz, gx, gy,
    ld, send, near_a, near_b, far_a, far_b, part_send, part_recv,
    gz_send, gz_recv, gx_send, gx_recv, gy_send, gy_recv, nz_send, nz_recv,
):
    rows = lax.axis_index("rows")
    model = lax.axis_index("model")
    z, core = rows // 2, rows % 2
    y, x = model // 4, model % 4
    up, down = (z + 1) % 4, (z + 3) % 4
    far = (z + 2) % 4
    right, left, above, below = (x + 1) % 4, (x + 3) % 4, (y + 1) % 4, (y + 3) % 4
    to_up = {"rows": up * 2 + core}
    to_down = {"rows": down * 2 + core}
    to_part = {"rows": z * 2 + 1 - core}
    to_far, to_zero = {"rows": far * 2 + core}, {"rows": core}
    to_right, to_left = {"model": y * 4 + right}, {"model": y * 4 + left}
    to_above, to_below = {"model": above * 4 + x}, {"model": below * 4 + x}

    barrier = pltpu.get_barrier_semaphore()
    for peer in (to_up, to_down, to_part):
        pl.semaphore_signal(barrier, inc=1, device_id=peer, device_id_type=MESH)

    @pl.when(z == 0)
    def _():
        for peer in (to_far, to_right, to_left, to_above, to_below):
            pl.semaphore_signal(barrier, inc=1, device_id=peer, device_id_type=MESH)

    @pl.when(z == 2)
    def _():
        pl.semaphore_signal(barrier, inc=1, device_id=to_far, device_id_type=MESH)

    loads = [
        (na, sna), (nb, snb), (tk, xk), (lk, slk), (hk, shk), (tv, xv), (lv, slv), (hv, shv),
        (lm, slm), (hm, shm), (tm, xm),
        (lq, slq), (hq, shq), (tq, xq),
    ]
    loads = [pltpu.make_async_copy(s, d, ld.at[i]) for i, (s, d) in enumerate(loads)]
    for c in loads:
        c.start()

    def low_rank(high, low):
        return mix_rate * lax.dot_general(
            high, low, (((0,), (0,)), ((), ())), preferred_element_type=jnp.float32
        )

    def make_narrow(k, base, high, low):
        for j in range(2):
            cols = pl.ds(j * 512, 512)
            b[rows, k, pl.ds(j * 64, 64), :] = (
                base[:, cols].astype(jnp.float32) + low_rank(high[...], low[:, cols])
            ).astype(jnp.bfloat16)

    def copy_to(src, index, send_sem, recv_sem, to):
        return pltpu.make_async_remote_copy(
            src_ref=b.at[src, index], dst_ref=b.at[src, index], send_sem=send_sem,
            recv_sem=recv_sem, device_id=to, device_id_type=MESH,
        )

    def gz_copy(chip, to):
        return pltpu.make_async_remote_copy(
            src_ref=gz.at[chip], dst_ref=gz.at[chip], send_sem=gz_send, recv_sem=gz_recv.at[chip],
            device_id=to, device_id_type=MESH,
        )

    def send_own(k):
        copy_to(rows, k, send.at[0], near_a.at[k], to_up).start()
        copy_to(rows, k, send.at[1], near_b.at[k], to_down).start()

    def to_partner(chip, k):
        copy_to(chip * 2 + core, k, part_send.at[chip], part_recv.at[chip], to_part).start()

    for c in loads[:5]:
        c.wait()
    gain = sna[...] + snb[...]
    gz[z] = jnp.concatenate([gain, gain], axis=1)
    make_narrow(0, xk, shk, slk)
    pl.when(z == 0)(lambda: pl.semaphore_wait(barrier, 8))
    pl.when(z == 2)(lambda: pl.semaphore_wait(barrier, 4))
    pl.when(z % 2 == 1)(lambda: pl.semaphore_wait(barrier, 3))

    @pl.when(z != 0)
    def _():
        gz_copy(z, to_zero).start()

    for c in loads[5:8]:
        c.wait()
    send_own(0)
    make_narrow(1, xv, shv, slv)
    for c in loads[8:]:
        c.wait()
    send_own(1)
    to_partner(z, 0)
    to_partner(z, 1)

    def make_query(i):
        left, top = (i // 4) * 512, (i % 4) * 128
        left, top = pl.multiple_of(left, 512), pl.multiple_of(top, 128)
        part = low_rank(shq[:, pl.ds(top, 128)], slq[:, pl.ds(left, 512)])
        base = xq[pl.ds(left, 512), pl.ds(top, 128)].astype(jnp.float32)
        b[rows, 2 + i] = (base.T + part).astype(jnp.bfloat16)

    def make_mixed(i):
        top = pl.multiple_of(i * 128, 128)
        part = low_rank(shm[:, pl.ds(top, 128)], slm[...])
        base = xm[:, pl.ds(top, 128)].astype(jnp.float32)
        b[rows, 10 + i] = (base.T + part).astype(jnp.bfloat16)

    make_query(0)

    @pl.loop(1, 8)
    def _(i):
        make_query(i)
        send_own(1 + i)
        to_partner(z, 1 + i)

    make_mixed(0)
    send_own(9)
    to_partner(z, 9)

    @pl.loop(1, 8)
    def _(i):
        make_mixed(i)
        send_own(9 + i)
        to_partner(z, 9 + i)

    def tile(ref, src, sems, k, to):
        return pltpu.make_async_remote_copy(
            src_ref=ref.at[src], dst_ref=ref.at[src], send_sem=sems[0].at[k], recv_sem=sems[1].at[k],
            device_id=to, device_id_type=MESH,
        )

    def both(ref, src, sems, one, other):
        return [tile(ref, src, sems, 0, one), tile(ref, src, sems, 1, other)]

    gx_sems, gy_sems, nz_sems = (gx_send, gx_recv), (gy_send, gy_recv), (nz_send, nz_recv)
    gx_near, gx_far = both(gx, x, gx_sems, to_right, to_left), tile(gx, left, gx_sems, 2, to_right)
    gy_near, gy_far = both(gy, y, gy_sems, to_above, to_below), tile(gy, below, gy_sems, 2, to_above)
    nz_part = tile(nz, core, nz_sems, 3, to_part)

    def nz_back(chip):
        return pltpu.make_async_remote_copy(
            src_ref=nz.at[core], dst_ref=nz.at[core], send_sem=nz_send.at[chip - 1], recv_sem=nz_recv.at[0],
            device_id={"rows": chip * 2 + core}, device_id_type=MESH,
        )

    def make_x():
        for i in range(1, 4):
            gz_copy(i, to_up).wait_recv()
        for i in range(4):
            gx[x, i : i + 1] = gz[i]

    def near_x():
        for c in gx_near:
            c.start()

    def far_x():
        for c in gx_near:
            c.wait()
        gx_far.start()

    def make_y():
        gx_far.wait()
        lane = lax.broadcasted_iota(jnp.int32, (4, 128), 1)
        gy[y, 0] = jnp.where(lane < 64, gx[0], gx[1])
        gy[y, 1] = jnp.where(lane < 64, gx[2], gx[3])

    def near_y():
        for c in gy_near:
            c.start()

    def far_y():
        for c in gy_near:
            c.wait()
        gy_far.start()

    def make_z():
        gy_far.wait()
        for i in range(4):
            for k in range(8):
                nz[core, i, k : k + 1] = gy[k // 2, k % 2, i : i + 1]

    def back_z():
        for i in range(1, 4):
            nz_back(i).start()

    gain_steps = [near_x, far_x, make_y, near_y, far_y, make_z, back_z]
    pl.when(z == 0)(make_x)
    send_own(17)
    to_partner(z, 17)

    def fourth(src, index, i, send_sem, recv_sem, to):
        part = b.at[src, index, pl.ds(i * 32, 32)]
        return pltpu.make_async_remote_copy(
            src_ref=part, dst_ref=part, send_sem=send_sem, recv_sem=recv_sem, device_id=to, device_id_type=MESH
        )

    def pass_on(src, j, send_sem, sems, to, index):
        if j < HALF - 1:
            copy_to(src, index, send_sem, sems.at[j], to).start()
        else:
            for i in range(4):
                fourth(src, index, i, send_sem, sems.at[j + i], to).start()

    below_chip, above_chip = down * 2 + core, up * 2 + core
    for k in range(PIECES):
        j = k // 2
        copy_to(below_chip, k, send.at[0], near_a.at[k], to_up).wait_recv()
        if k % 2 == 0:
            pass_on(below_chip, j, send.at[2], far_a, to_up, k)
        to_partner(down, k)
        copy_to(above_chip, k, send.at[1], near_b.at[k], to_down).wait_recv()
        if k % 2 == 1:
            pass_on(above_chip, j, send.at[3], far_b, to_down, k)
        to_partner(up, k)
        if k < len(gain_steps):
            pl.when(z == 0)(gain_steps[k])

    far_chip = far * 2 + core

    def far_pieces(first, last):
        @pl.loop(first, last)
        def _(j):
            copy_to(far_chip, 2 * j, send.at[2], far_a.at[j], to_up).wait_recv()
            to_partner(far, 2 * j)
            copy_to(far_chip, 2 * j + 1, send.at[3], far_b.at[j], to_down).wait_recv()
            to_partner(far, 2 * j + 1)

    far_pieces(0, 5)

    @pl.when(z != 0)
    def _():
        gz_copy(z, to_zero).wait_send()
        nz_back(1).wait_recv()

    @pl.when(z == 0)
    def _():
        for i in range(1, 4):
            nz_back(i).wait_send()

    nz_part.start()
    far_pieces(5, HALF - 1)
    nz_part.wait()

    def all_of(src, count, send_sem, recv_sem, to):
        part = b.at[src, pl.ds(0, count)]
        return pltpu.make_async_remote_copy(
            src_ref=part, dst_ref=part, send_sem=send_sem, recv_sem=recv_sem,
            device_id=to, device_id_type=MESH,
        )

    for i in range(4):
        for index, sems, sem, to in ((16, far_a, send.at[2], to_up), (17, far_b, send.at[3], to_down)):
            fourth(far_chip, index, i, sem, sems.at[HALF - 1 + i], to).wait_recv()
            fourth(far_chip, index, i, part_send.at[far], part_recv.at[far], to_part).start()

    all_of(rows, PIECES, send.at[0], near_a.at[0], to_up).wait_send()
    all_of(rows, PIECES, send.at[1], near_b.at[0], to_down).wait_send()
    all_of(rows, HALF, send.at[2], far_a.at[0], to_up).wait_send()
    all_of(rows, HALF, send.at[3], far_b.at[0], to_down).wait_send()
    for c in range(4):
        all_of(c * 2 + core, PIECES, part_send.at[c], part_recv.at[c], to_part).wait_send()
        all_of(c * 2 + 1 - core, PIECES, part_send.at[c], part_recv.at[c], to_part).wait_recv()


def comm(*args):
    bf16, f32 = jnp.bfloat16, jnp.float32
    dma = pltpu.SemaphoreType.DMA
    return pl.pallas_call(
        comm_kernel,
        out_shape=[pltpu.VMEM((8, PIECES, 128, 512), bf16), pltpu.VMEM((2, 4, 8, 128), f32)],
        in_specs=[HBM] * len(args),
        out_specs=[VMEM] * 2,
        scratch_shapes=[
            pltpu.VMEM((1024, 512), bf16), pltpu.VMEM((64, 1024), bf16), pltpu.VMEM((64, 1024), bf16),
            pltpu.VMEM((512, 1024), bf16),
            pltpu.VMEM((16, 1024), bf16), pltpu.VMEM((16, 512), bf16),
            pltpu.VMEM((16, 1024), bf16), pltpu.VMEM((16, 64), bf16),
            pltpu.VMEM((16, 1024), bf16), pltpu.VMEM((16, 64), bf16),
            pltpu.VMEM((16, 512), bf16), pltpu.VMEM((16, 1024), bf16),
            pltpu.VMEM((1, 64), f32), pltpu.VMEM((1, 64), f32),
            pltpu.VMEM((4, 1, 128), f32), pltpu.VMEM((4, 4, 128), f32), pltpu.VMEM((4, 2, 4, 128), f32),
            dma((14,)), dma((4,)), dma((PIECES,)), dma((PIECES,)), dma((HALF + 3,)), dma((HALF + 3,)),
            dma((4,)), dma((4,)),
            dma, dma((4,)), dma((3,)), dma((3,)), dma((3,)), dma((3,)), dma((4,)), dma((4,)),
        ],
        compiler_params=pltpu.CompilerParams(
            collective_id=0, has_side_effects=True, vmem_limit_bytes=44 * 2**20
        ),
        name="comm",
    )(*args)


def write_kernel(b, nz, q, k, v, m, n, gain, sem):
    tiles = [nz[r % 2, r // 2] for r in range(8)]
    gain[...] = jnp.concatenate(tiles, axis=0).astype(jnp.bfloat16)
    for r in range(8):
        for j in range(2):
            cols, half = pl.ds(r * 1024 + j * 512, 512), pl.ds(j * 64, 64)
            pltpu.make_async_copy(b.at[r, 0, half], k.at[:, cols], sem.at[0]).start()
            pltpu.make_async_copy(b.at[r, 1, half], v.at[:, cols], sem.at[1]).start()
    for r in range(8):
        pltpu.make_async_copy(b.at[r, pl.ds(10, 8)], m.at[pl.ds(r * 8, 8)], sem.at[3]).start()
        for j in range(2):
            cols = pl.ds(r * 1024 + j * 512, 512)
            pltpu.make_async_copy(b.at[r, pl.ds(2 + 4 * j, 4)], q.at[:, :, cols], sem.at[2]).start()
    pltpu.make_async_copy(gain, n, sem.at[4]).start()
    for i, ref in enumerate((k, v, q, m, n)):
        pltpu.make_async_copy(ref, ref, sem.at[i]).wait()


def write(b, nz):
    bf16 = jnp.bfloat16
    shapes = [(4, 128, 8192), (64, 8192), (64, 8192), (64, 128, 512), (64, 128)]
    return pl.pallas_call(
        write_kernel,
        out_shape=[jax.ShapeDtypeStruct(s, bf16) for s in shapes],
        in_specs=[VMEM] * 2,
        out_specs=[HBM] * 5,
        scratch_shapes=[pltpu.VMEM((64, 128), bf16), pltpu.SemaphoreType.DMA((5,))],
        compiler_params=pltpu.CompilerParams(vmem_limit_bytes=4 * 2**20),
        name="write",
    )(b, nz)


def body(
    train_query, low_query, high_query, train_key, low_key, high_key, train_value, low_value, high_value,
    train_mixed, low_mixed, high_mixed, norm_train, norm_step,
):
    b, nz = comm(
        train_query, train_key.T, train_value.T, train_mixed,
        low_query.T, high_query, low_key.T, high_key, low_value.T, high_value, low_mixed.T, high_mixed,
        norm_train.reshape(1, 64), norm_step.reshape(1, 64),
    )
    q, k, v, m, n = write(b, nz)
    return q.reshape(512, 8192), k, v, m.reshape(8192, 512), n.reshape(8192)


def solution(mesh):
    R, M = "rows", "model"
    return jax.shard_map(
        body,
        mesh=mesh,
        in_specs=(
            P(R, M), P(R, None), P(None, M),
            P(R, M), P(R, None), P(None, M),
            P(R, M), P(R, None), P(None, M),
            P(M, R), P(M, None), P(None, R),
            P((R, M)), P((R, M)),
        ),
        out_specs=(P(M, None), P(M, None), P(M, None), P(None, M), P()),
        check_vma=False,
    )
```

time: 95.1 us -> 92.4 us (0.972)
  Pallas kernels: 94.3 us -> 91.6 us
    pallas_call x1, Pallas kernels: 87.3 us -> 85.1 us  [comm(): pl.pallas_call(comm_kernel, out_shape=[pltpu.VMEM((8, PIECES, 128, 512),...]
where the time goes in v2:
time: 92.4 us; the launch traced here: 92.2 us
  Pallas kernels  91.6 us (99%)
    pallas_call x1, Pallas kernels, comm(): pl.pallas_call(comm_kernel, out_shape=[pltpu.VMEM((8, PIECES, 128, 512),...  85.1 us
    pallas_call x1, Pallas kernels, write(): pl.pallas_call(write_kernel, out_shape=[jax.ShapeDtypeStruct(s, bf16) for...  6.46 us

profile of v2, /device:TPU:1, one launch (start us, length us, event | category | flops | bytes accessed | tf_op | source)
XLA Modules:
  0.0 92.2 jit_solution(7617221278251776857)
XLA Ops:
  0.6 85.1 %comm.1 = (bf16[8,18,128,512]{3,2,1,0:T(8,128)(2,1)S(1)}, f32[2,4,8,128]{3,2,1,0:T(8,128)S(1)}) custom-call(bf16[1024,512]{1,0:T(8,128)(2,1)} %tq.1, bf16[64,1024]{1,0:T(8,128)(2,1)} %bitcast.11, bf16[64,1024]{1,0:T(8,128)(2,1)} %bitcast.12, bf16[512,1024]{1,0:T(8,128)(2,1)} %tm.1, bf16[16,1024]{1,0:T(8,128)(2,1)} %bitcast.13, bf16[16,512]{1,0:T(8,128)(2,1)} %hq.1, ...), custom_call_target="tpu_custom_call" | custom-call | tf_op jit(solution)/shard_map/comm/pallas_call | solution.py:288
  85.8 6.5 %write.1 = (bf16[4,128,8192]{2,1,0:T(8,128)(2,1)}, bf16[64,8192]{1,0:T(8,128)(2,1)}, bf16[64,8192]{1,0:T(8,128)(2,1)}, bf16[64,128,512]{2,1,0:T(8,128)(2,1)}, bf16[64,128]{1,0:T(8,128)(2,1)}) custom-call(bf16[8,18,128,512]{3,2,1,0:T(8,128)(2,1)S(1)} %get-tuple-element.12.b, f32[2,4,8,128]{3,2,1,0:T(8,128)S(1)} %get-tuple-element.13.nz), custom_call_target="tpu_custom_call" | custom-call | tf_op jit(solution)/shard_map/write/pallas_call | solution.py:334

commit v3 on v2

--- a/solution.py
+++ b/solution.py
@@ -12,15 +12,19 @@
 mix_rate = 0.5
 
 PIECES = 18
-HALF = PIECES // 2
+
+SPLIT = 96
+WAY_UP = ((0, 0, SPLIT),)
+WAY_DOWN = ((0, SPLIT, 128 - SPLIT), (1, 0, 128)) if SPLIT < 128 else ((1, 0, 128),)
 
 
 def comm_kernel(
     tq, tk, tv, tm, lq, hq, lk, hk, lv, hv, lm, hm, na, nb,
-    b, nz,
+    b, late, nz,
     xq, xk, xv, xm, slq, shq, slk, shk, slv, shv, slm, shm, sna, snb, gz, gx, gy,
     ld, send, near_a, near_b, far_a, far_b, part_send, part_recv,
     gz_send, gz_recv, gx_send, gx_recv, gy_send, gy_recv, nz_send, nz_recv,
+    late_send, late_recv,
 ):
     rows = lax.axis_index("rows")
     model = lax.axis_index("model")
@@ -208,34 +212,36 @@
     send_own(17)
     to_partner(z, 17)
 
-    def fourth(src, index, i, send_sem, recv_sem, to):
-        part = b.at[src, index, pl.ds(i * 32, 32)]
-        return pltpu.make_async_remote_copy(
-            src_ref=part, dst_ref=part, send_sem=send_sem, recv_sem=recv_sem, device_id=to, device_id_type=MESH
-        )
-
-    def pass_on(src, j, send_sem, sems, to, index):
-        if j < HALF - 1:
-            copy_to(src, index, send_sem, sems.at[j], to).start()
-        else:
-            for i in range(4):
-                fourth(src, index, i, send_sem, sems.at[j + i], to).start()
+    def pass_on(k, src):
+        way, sem, to = ((2, far_a, to_up), (3, far_b, to_down))[k % 2]
+        return copy_to(src, k, send.at[way], sem.at[k // 2], to)
+
+    def pass_late(way, n, src):
+        (piece, first, count), to = ((WAY_UP, WAY_DOWN)[way][n], (to_up, to_down)[way])
+        some = pl.ds(first, count)
+        return pltpu.make_async_remote_copy(
+            src_ref=b.at[src, piece, some], dst_ref=late.at[piece, some], send_sem=late_send.at[way, n],
+            recv_sem=late_recv.at[way, n], device_id=to, device_id_type=MESH,
+        )
 
     below_chip, above_chip = down * 2 + core, up * 2 + core
+    far_chip = far * 2 + core
     for k in range(PIECES):
-        j = k // 2
         copy_to(below_chip, k, send.at[0], near_a.at[k], to_up).wait_recv()
-        if k % 2 == 0:
-            pass_on(below_chip, j, send.at[2], far_a, to_up, k)
+        if k >= 2 and k % 2 == 0:
+            pass_on(k, below_chip).start()
         to_partner(down, k)
         copy_to(above_chip, k, send.at[1], near_b.at[k], to_down).wait_recv()
-        if k % 2 == 1:
-            pass_on(above_chip, j, send.at[3], far_b, to_down, k)
+        if k >= 2 and k % 2 == 1:
+            pass_on(k, above_chip).start()
         to_partner(up, k)
         if k < len(gain_steps):
             pl.when(z == 0)(gain_steps[k])
 
-    far_chip = far * 2 + core
+    late_copies = [pass_late(0, n, below_chip) for n in range(len(WAY_UP))]
+    late_copies += [pass_late(1, n, above_chip) for n in range(len(WAY_DOWN))]
+    for c in late_copies:
+        c.start()
 
     def far_pieces(first, last):
         @pl.loop(first, last)
@@ -245,7 +251,7 @@
             copy_to(far_chip, 2 * j + 1, send.at[3], far_b.at[j], to_down).wait_recv()
             to_partner(far, 2 * j + 1)
 
-    far_pieces(0, 5)
+    far_pieces(1, 6)
 
     @pl.when(z != 0)
     def _():
@@ -258,7 +264,7 @@
             nz_back(i).wait_send()
 
     nz_part.start()
-    far_pieces(5, HALF - 1)
+    far_pieces(6, 9)
     nz_part.wait()
 
     def all_of(src, count, send_sem, recv_sem, to):
@@ -268,18 +274,15 @@
             device_id=to, device_id_type=MESH,
         )
 
-    for i in range(4):
-        for index, sems, sem, to in ((16, far_a, send.at[2], to_up), (17, far_b, send.at[3], to_down)):
-            fourth(far_chip, index, i, sem, sems.at[HALF - 1 + i], to).wait_recv()
-            fourth(far_chip, index, i, part_send.at[far], part_recv.at[far], to_part).start()
-
     all_of(rows, PIECES, send.at[0], near_a.at[0], to_up).wait_send()
     all_of(rows, PIECES, send.at[1], near_b.at[0], to_down).wait_send()
-    all_of(rows, HALF, send.at[2], far_a.at[0], to_up).wait_send()
-    all_of(rows, HALF, send.at[3], far_b.at[0], to_down).wait_send()
-    for c in range(4):
-        all_of(c * 2 + core, PIECES, part_send.at[c], part_recv.at[c], to_part).wait_send()
-        all_of(c * 2 + 1 - core, PIECES, part_send.at[c], part_recv.at[c], to_part).wait_recv()
+    all_of(rows, 8, send.at[2], far_a.at[0], to_up).wait_send()
+    all_of(rows, 8, send.at[3], far_b.at[0], to_down).wait_send()
+    for chip, count in ((z, PIECES), (up, PIECES), (down, PIECES), (far, PIECES - 2)):
+        all_of(chip * 2 + core, count, part_send.at[chip], part_recv.at[chip], to_part).wait_send()
+        all_of(chip * 2 + 1 - core, count, part_send.at[chip], part_recv.at[chip], to_part).wait_recv()
+    for c in late_copies:
+        c.wait()
 
 
 def comm(*args):
@@ -287,9 +290,11 @@
     dma = pltpu.SemaphoreType.DMA
     return pl.pallas_call(
         comm_kernel,
-        out_shape=[pltpu.VMEM((8, PIECES, 128, 512), bf16), pltpu.VMEM((2, 4, 8, 128), f32)],
+        out_shape=[
+            pltpu.VMEM((8, PIECES, 128, 512), bf16), pltpu.VMEM((2, 128, 512), bf16), pltpu.VMEM((2, 4, 8, 128), f32),
+        ],
         in_specs=[HBM] * len(args),
-        out_specs=[VMEM] * 2,
+        out_specs=[VMEM] * 3,
         scratch_shapes=[
             pltpu.VMEM((1024, 512), bf16), pltpu.VMEM((64, 1024), bf16), pltpu.VMEM((64, 1024), bf16),
             pltpu.VMEM((512, 1024), bf16),
@@ -299,9 +304,10 @@
             pltpu.VMEM((16, 512), bf16), pltpu.VMEM((16, 1024), bf16),
             pltpu.VMEM((1, 64), f32), pltpu.VMEM((1, 64), f32),
             pltpu.VMEM((4, 1, 128), f32), pltpu.VMEM((4, 4, 128), f32), pltpu.VMEM((4, 2, 4, 128), f32),
-            dma((14,)), dma((4,)), dma((PIECES,)), dma((PIECES,)), dma((HALF + 3,)), dma((HALF + 3,)),
+            dma((14,)), dma((4,)), dma((PIECES,)), dma((PIECES,)), dma((PIECES // 2,)), dma((PIECES // 2,)),
             dma((4,)), dma((4,)),
             dma, dma((4,)), dma((3,)), dma((3,)), dma((3,)), dma((3,)), dma((4,)), dma((4,)),
+            dma((2, 2)), dma((2, 2)),
         ],
         compiler_params=pltpu.CompilerParams(
             collective_id=0, has_side_effects=True, vmem_limit_bytes=44 * 2**20
@@ -310,48 +316,81 @@
     )(*args)
 
 
-def write_kernel(b, nz, q, k, v, m, n, gain, sem):
+def put_narrow(r, block, k, v, sem):
+    for i, out in enumerate((k, v)):
+        for j in range(2):
+            cols = pl.ds(pl.multiple_of(r * 1024 + j * 512, 512), 512)
+            pltpu.make_async_copy(block.at[i, pl.ds(j * 64, 64)], out.at[:, cols], sem.at[i]).start()
+
+
+def write_kernel(b, late, nz, q, k, v, m, n, gain, sem):
     tiles = [nz[r % 2, r // 2] for r in range(8)]
     gain[...] = jnp.concatenate(tiles, axis=0).astype(jnp.bfloat16)
-    for r in range(8):
-        for j in range(2):
-            cols, half = pl.ds(r * 1024 + j * 512, 512), pl.ds(j * 64, 64)
-            pltpu.make_async_copy(b.at[r, 0, half], k.at[:, cols], sem.at[0]).start()
-            pltpu.make_async_copy(b.at[r, 1, half], v.at[:, cols], sem.at[1]).start()
     for r in range(8):
         pltpu.make_async_copy(b.at[r, pl.ds(10, 8)], m.at[pl.ds(r * 8, 8)], sem.at[3]).start()
         for j in range(2):
             cols = pl.ds(r * 1024 + j * 512, 512)
             pltpu.make_async_copy(b.at[r, pl.ds(2 + 4 * j, 4)], q.at[:, :, cols], sem.at[2]).start()
+    rows = lax.axis_index("rows")
+    core = rows % 2
+    far = (rows // 2 + 2) % 4 * 2
+    for d in range(2, 8):
+        r = (far + d) % 8
+        put_narrow(r, b.at[r, pl.ds(0, 2)], k, v, sem)
+    put_narrow(far + core, late, k, v, sem)
     pltpu.make_async_copy(gain, n, sem.at[4]).start()
-    for i, ref in enumerate((k, v, q, m, n)):
+    for i, ref in enumerate((k.at[:, pl.ds(0, 7168)], v.at[:, pl.ds(0, 7168)], q, m, n)):
         pltpu.make_async_copy(ref, ref, sem.at[i]).wait()
 
 
-def write(b, nz):
+def write(b, late, nz):
     bf16 = jnp.bfloat16
     shapes = [(4, 128, 8192), (64, 8192), (64, 8192), (64, 128, 512), (64, 128)]
     return pl.pallas_call(
         write_kernel,
         out_shape=[jax.ShapeDtypeStruct(s, bf16) for s in shapes],
-        in_specs=[VMEM] * 2,
+        in_specs=[VMEM] * 3,
         out_specs=[HBM] * 5,
         scratch_shapes=[pltpu.VMEM((64, 128), bf16), pltpu.SemaphoreType.DMA((5,))],
         compiler_params=pltpu.CompilerParams(vmem_limit_bytes=4 * 2**20),
+        cost_estimate=pl.CostEstimate(flops=0, bytes_accessed=38 * 2**20, transcendentals=0),
         name="write",
-    )(b, nz)
+    )(b, late, nz)
+
+
+def last_kernel(other, k_in, v_in, k, v, sem):
+    rows = lax.axis_index("rows")
+    put_narrow((rows // 2 + 2) % 4 * 2 + 1 - rows % 2, other, k, v, sem)
+    for i, ref in enumerate((k, v)):
+        part = ref.at[:, pl.ds(0, 1024)]
+        pltpu.make_async_copy(part, part, sem.at[i]).wait()
+
+
+def write_last(other, k, v):
+    return pl.pallas_call(
+        last_kernel,
+        out_shape=[jax.ShapeDtypeStruct(a.shape, a.dtype) for a in (k, v)],
+        in_specs=[VMEM, HBM, HBM],
+        out_specs=[HBM] * 2,
+        scratch_shapes=[pltpu.SemaphoreType.DMA((2,))],
+        input_output_aliases={1: 0, 2: 1},
+        compiler_params=pltpu.CompilerParams(vmem_limit_bytes=2**20),
+        name="write_last",
+    )(other, k, v)
 
 
 def body(
     train_query, low_query, high_query, train_key, low_key, high_key, train_value, low_value, high_value,
     train_mixed, low_mixed, high_mixed, norm_train, norm_step,
 ):
-    b, nz = comm(
+    b, late, nz = comm(
         train_query, train_key.T, train_value.T, train_mixed,
         low_query.T, high_query, low_key.T, high_key, low_value.T, high_value, low_mixed.T, high_mixed,
         norm_train.reshape(1, 64), norm_step.reshape(1, 64),
     )
-    q, k, v, m, n = write(b, nz)
+    other = lax.ppermute(late, "rows", [(r, r + 1 - 2 * (r % 2)) for r in range(8)])
+    q, k, v, m, n = write(b, late, nz)
+    k, v = write_last(other, k, v)
     return q.reshape(512, 8192), k, v, m.reshape(8192, 512), n.reshape(8192)
 
 

time: 92.4 us -> 91.7 us (level)
  Pallas kernels: 91.6 us -> 90.6 us
    pallas_call x1, Pallas kernels: 85.1 us -> 83.5 us  [comm(): pl.pallas_call(comm_kernel, out_shape=[pltpu.VMEM((8, PIECES, 128, 512),...]
  transfers between devices with their start and end apart: 0 -> 1, of which waited for: 0 -> 0; matrix products, arithmetic and copies ran while one was open for 0% -> 0% of each run, Pallas kernels for 0% -> 7%
where the time goes in v3:
time: 91.7 us; the launch traced here: 91.5 us
  Pallas kernels  90.6 us (99%)
    pallas_call x1, Pallas kernels, comm(): pl.pallas_call(comm_kernel, out_shape=[pltpu.VMEM((8, PIECES, 128, 512),...  83.5 us
    pallas_call x1, Pallas kernels, write(): pl.pallas_call(write_kernel, out_shape=[jax.ShapeDtypeStruct(s, bf16) for...  6.36 us
  transfers between devices with their start and end apart: 1, of which 0 were waited for; matrix products, arithmetic and copies ran while one was open for 0% of the time, Pallas kernels for 7%

profile of v3, /device:TPU:1, one launch (start us, length us, event | category | flops | bytes accessed | tf_op | source)
XLA Modules:
  0.0 91.5 jit_solution(10250036631367383460)
XLA Ops:
  0.6 83.5 %comm.1 = (bf16[8,18,128,512]{3,2,1,0:T(8,128)(2,1)S(1)}, bf16[2,128,512]{2,1,0:T(8,128)(2,1)S(1)}, f32[2,4,8,128]{3,2,1,0:T(8,128)S(1)}) custom-call(bf16[1024,512]{1,0:T(8,128)(2,1)} %tq.1, bf16[64,1024]{1,0:T(8,128)(2,1)} %bitcast.11, bf16[64,1024]{1,0:T(8,128)(2,1)} %bitcast.12, bf16[512,1024]{1,0:T(8,128)(2,1)} %tm.1, bf16[16,1024]{1,0:T(8,128)(2,1)} %bitcast.13, ...), custom_call_target="tpu_custom_call" | custom-call | tf_op jit(solution)/shard_map/comm/pallas_call | solution.py:291
  84.1 0.3 collective-permute-start
  84.4 6.4 %write.1 = (bf16[4,128,8192]{2,1,0:T(8,128)(2,1)}, bf16[64,8192]{1,0:T(8,128)(2,1)}, bf16[64,8192]{1,0:T(8,128)(2,1)}, bf16[64,128,512]{2,1,0:T(8,128)(2,1)}, bf16[64,128]{1,0:T(8,128)(2,1)}) custom-call(bf16[8,18,128,512]{3,2,1,0:T(8,128)(2,1)S(1)} %get-tuple-element.15.b, bf16[2,128,512]{2,1,0:T(8,128)(2,1)S(1)} %get-tuple-element.16.late, ...), custom_call_target="tpu_custom_call" | custom-call | bytes 39845888 | tf_op jit(solution)/shard_map/write/pallas_call | solution.py:349
  90.8 0.0 collective-permute-done.other
  90.8 0.7 write_last.1
Async XLA Ops:
  84.1 6.7 %collective-permute-start = (bf16[2,128,512]{2,1,0:T(8,128)(2,1)S(1)}, bf16[2,128,512]{2,1,0:T(8,128)(2,1)S(1)}, u32[]{:S(2)}, u32[]{:S(2)}) collective-permute-start(bf16[2,128,512]{2,1,0:T(8,128)(2,1)S(1)} %get-tuple-element.16.late), channel_id=1, source_target_pairs={{0,16},{16,0},{32,48},{48,32},{64,80},{80,64},{96,112},{112,96},{1... | collective-permute-start | bytes 786440 | tf_op jit(solution)/shard_map/ppermute | solution.py:391

commit v4 on v3

--- a/solution.py
+++ b/solution.py
@@ -24,7 +24,7 @@
     xq, xk, xv, xm, slq, shq, slk, shk, slv, shv, slm, shm, sna, snb, gz, gx, gy,
     ld, send, near_a, near_b, far_a, far_b, part_send, part_recv,
     gz_send, gz_recv, gx_send, gx_recv, gy_send, gy_recv, nz_send, nz_recv,
-    late_send, late_recv,
+    late_send, late_recv, early_send, early_recv,
 ):
     rows = lax.axis_index("rows")
     model = lax.axis_index("model")
@@ -93,6 +93,9 @@
     def to_partner(chip, k):
         copy_to(chip * 2 + core, k, part_send.at[chip], part_recv.at[chip], to_part).start()
 
+    def early(chip, k):
+        return copy_to(chip * 2 + core, k, early_send.at[chip, k], early_recv.at[chip, k], to_part)
+
     for c in loads[:5]:
         c.wait()
     gain = sna[...] + snb[...]
@@ -216,12 +219,12 @@
         way, sem, to = ((2, far_a, to_up), (3, far_b, to_down))[k % 2]
         return copy_to(src, k, send.at[way], sem.at[k // 2], to)
 
-    def pass_late(way, n, src):
+    def pass_late(way, n, of):
         (piece, first, count), to = ((WAY_UP, WAY_DOWN)[way][n], (to_up, to_down)[way])
         some = pl.ds(first, count)
         return pltpu.make_async_remote_copy(
-            src_ref=b.at[src, piece, some], dst_ref=late.at[piece, some], send_sem=late_send.at[way, n],
-            recv_sem=late_recv.at[way, n], device_id=to, device_id_type=MESH,
+            src_ref=b.at[(down, up)[way] * 2 + of, piece, some], dst_ref=late.at[of, piece, some],
+            send_sem=late_send.at[of, way, n], recv_sem=late_recv.at[of, way, n], device_id=to, device_id_type=MESH,
         )
 
     below_chip, above_chip = down * 2 + core, up * 2 + core
@@ -230,18 +233,24 @@
         copy_to(below_chip, k, send.at[0], near_a.at[k], to_up).wait_recv()
         if k >= 2 and k % 2 == 0:
             pass_on(k, below_chip).start()
-        to_partner(down, k)
+        early(down, k).start() if k < 2 else to_partner(down, k)
         copy_to(above_chip, k, send.at[1], near_b.at[k], to_down).wait_recv()
         if k >= 2 and k % 2 == 1:
             pass_on(k, above_chip).start()
-        to_partner(up, k)
+        early(up, k).start() if k < 2 else to_partner(up, k)
         if k < len(gain_steps):
             pl.when(z == 0)(gain_steps[k])
 
-    late_copies = [pass_late(0, n, below_chip) for n in range(len(WAY_UP))]
-    late_copies += [pass_late(1, n, above_chip) for n in range(len(WAY_DOWN))]
-    for c in late_copies:
-        c.start()
+    for chip in (down, up):
+        for k in range(2):
+            early(chip, k).wait()
+    late_parts = [(0, n, of) for n in range(len(WAY_UP)) for of in range(2)]
+    late_parts += [(1, n, of) for n in range(len(WAY_DOWN)) for of in range(2)]
+
+    @pl.when(core == 1)
+    def _():
+        for part in late_parts:
+            pass_late(*part).start()
 
     def far_pieces(first, last):
         @pl.loop(first, last)
@@ -278,11 +287,14 @@
     all_of(rows, PIECES, send.at[1], near_b.at[0], to_down).wait_send()
     all_of(rows, 8, send.at[2], far_a.at[0], to_up).wait_send()
     all_of(rows, 8, send.at[3], far_b.at[0], to_down).wait_send()
-    for chip, count in ((z, PIECES), (up, PIECES), (down, PIECES), (far, PIECES - 2)):
+    for chip, count in ((z, PIECES), (up, PIECES - 2), (down, PIECES - 2), (far, PIECES - 2)):
         all_of(chip * 2 + core, count, part_send.at[chip], part_recv.at[chip], to_part).wait_send()
         all_of(chip * 2 + 1 - core, count, part_send.at[chip], part_recv.at[chip], to_part).wait_recv()
-    for c in late_copies:
-        c.wait()
+
+    @pl.when(core == 1)
+    def _():
+        for part in late_parts:
+            pass_late(*part).wait()
 
 
 def comm(*args):
@@ -291,7 +303,8 @@
     return pl.pallas_call(
         comm_kernel,
         out_shape=[
-            pltpu.VMEM((8, PIECES, 128, 512), bf16), pltpu.VMEM((2, 128, 512), bf16), pltpu.VMEM((2, 4, 8, 128), f32),
+            pltpu.VMEM((8, PIECES, 128, 512), bf16), pltpu.VMEM((2, 2, 128, 512), bf16),
+            pltpu.VMEM((2, 4, 8, 128), f32),
         ],
         in_specs=[HBM] * len(args),
         out_specs=[VMEM] * 3,
@@ -307,7 +320,7 @@
             dma((14,)), dma((4,)), dma((PIECES,)), dma((PIECES,)), dma((PIECES // 2,)), dma((PIECES // 2,)),
             dma((4,)), dma((4,)),
             dma, dma((4,)), dma((3,)), dma((3,)), dma((3,)), dma((3,)), dma((4,)), dma((4,)),
-            dma((2, 2)), dma((2, 2)),
+            dma((2, 2, 2)), dma((2, 2, 2)), dma((4, 2)), dma((4, 2)),
         ],
         compiler_params=pltpu.CompilerParams(
             collective_id=0, has_side_effects=True, vmem_limit_bytes=44 * 2**20
@@ -337,10 +350,25 @@
     for d in range(2, 8):
         r = (far + d) % 8
         put_narrow(r, b.at[r, pl.ds(0, 2)], k, v, sem)
-    put_narrow(far + core, late, k, v, sem)
     pltpu.make_async_copy(gain, n, sem.at[4]).start()
-    for i, ref in enumerate((k.at[:, pl.ds(0, 7168)], v.at[:, pl.ds(0, 7168)], q, m, n)):
+
+    def wait(i, ref):
         pltpu.make_async_copy(ref, ref, sem.at[i]).wait()
+
+    @pl.when(core == 1)
+    def _():
+        for of in range(2):
+            put_narrow(far + of, late.at[of], k, v, sem)
+        wait(0, k)
+        wait(1, v)
+
+    @pl.when(core == 0)
+    def _():
+        wait(0, k.at[:, pl.ds(0, 6144)])
+        wait(1, v.at[:, pl.ds(0, 6144)])
+
+    for i, ref in ((2, q), (3, m), (4, n)):
+        wait(i, ref)
 
 
 def write(b, late, nz):
@@ -360,10 +388,15 @@
 
 def last_kernel(other, k_in, v_in, k, v, sem):
     rows = lax.axis_index("rows")
-    put_narrow((rows // 2 + 2) % 4 * 2 + 1 - rows % 2, other, k, v, sem)
-    for i, ref in enumerate((k, v)):
-        part = ref.at[:, pl.ds(0, 1024)]
-        pltpu.make_async_copy(part, part, sem.at[i]).wait()
+    far = (rows // 2 + 2) % 4 * 2
+
+    @pl.when(rows % 2 == 0)
+    def _():
+        for of in range(2):
+            put_narrow(far + of, other.at[of], k, v, sem)
+        for i, ref in enumerate((k, v)):
+            part = ref.at[:, pl.ds(0, 2048)]
+            pltpu.make_async_copy(part, part, sem.at[i]).wait()
 
 
 def write_last(other, k, v):

time: 91.7 us -> 91.2 us (level)
  no operation moved by 1% of the time
where the time goes in v4:
time: 91.2 us; the launch traced here: 91.1 us
  Pallas kernels  90.2 us (99%)
    pallas_call x1, Pallas kernels, comm(): pl.pallas_call(comm_kernel, out_shape=[pltpu.VMEM((8, PIECES, 128, 512),...  83.7 us
    pallas_call x1, Pallas kernels, write(): pl.pallas_call(write_kernel, out_shape=[jax.ShapeDtypeStruct(s, bf16) for...  6.44 us
  transfers between devices with their start and end apart: 1, of which 0 were waited for; matrix products, arithmetic and copies ran while one was open for 0% of the time, Pallas kernels for 7%

profile of v4, /device:TPU:1, one launch (start us, length us, event | category | flops | bytes accessed | tf_op | source)
XLA Modules:
  0.0 91.1 jit_solution(2089919990598043955)
XLA Ops:
  0.6 83.7 %comm.1 = (bf16[8,18,128,512]{3,2,1,0:T(8,128)(2,1)S(1)}, bf16[2,2,128,512]{3,2,1,0:T(8,128)(2,1)S(1)}, f32[2,4,8,128]{3,2,1,0:T(8,128)S(1)}) custom-call(bf16[1024,512]{1,0:T(8,128)(2,1)} %tq.1, bf16[64,1024]{1,0:T(8,128)(2,1)} %bitcast.11, bf16[64,1024]{1,0:T(8,128)(2,1)} %bitcast.12, bf16[512,1024]{1,0:T(8,128)(2,1)} %tm.1, bf16[16,1024]{1,0:T(8,128)(2,1)} %bitcast.13, ...), custom_call_target="tpu_custom_call" | custom-call | tf_op jit(solution)/shard_map/comm/pallas_call | solution.py:303
  84.3 0.2 collective-permute-start
  84.5 6.4 %write.1 = (bf16[4,128,8192]{2,1,0:T(8,128)(2,1)}, bf16[64,8192]{1,0:T(8,128)(2,1)}, bf16[64,8192]{1,0:T(8,128)(2,1)}, bf16[64,128,512]{2,1,0:T(8,128)(2,1)}, bf16[64,128]{1,0:T(8,128)(2,1)}) custom-call(bf16[8,18,128,512]{3,2,1,0:T(8,128)(2,1)S(1)} %get-tuple-element.15.b, bf16[2,2,128,512]{3,2,1,0:T(8,128)(2,1)S(1)} %get-tuple-element.16.late, ...), custom_call_target="tpu_custom_call" | custom-call | bytes 39845888 | tf_op jit(solution)/shard_map/write/pallas_call | solution.py:377
  91.0 0.0 collective-permute-done.other
  91.0 0.1 write_last.1
Async XLA Ops:
  84.3 6.7 %collective-permute-start = (bf16[2,2,128,512]{3,2,1,0:T(8,128)(2,1)S(1)}, bf16[2,2,128,512]{3,2,1,0:T(8,128)(2,1)S(1)}, u32[]{:S(2)}, u32[]{:S(2)}) collective-permute-start(bf16[2,2,128,512]{3,2,1,0:T(8,128)(2,1)S(1)} %get-tuple-element.16.late), channel_id=1, source_target_pairs={{0,16},{16,0},{32,48},{48,32},{64,80},{80,64},{96,112},{112,96},{1... | collective-permute-start | bytes 1572872 | tf_op jit(solution)/shard_map/ppermute | solution.py:424

commit v5 on v4

--- a/solution.py
+++ b/solution.py
@@ -13,7 +13,7 @@
 
 PIECES = 18
 
-SPLIT = 96
+SPLIT = 112
 WAY_UP = ((0, 0, SPLIT),)
 WAY_DOWN = ((0, SPLIT, 128 - SPLIT), (1, 0, 128)) if SPLIT < 128 else ((1, 0, 128),)
 

time: 91.2 us -> 91.2 us (level)
  no operation moved by 1% of the time
where the time goes in v5:
time: 91.2 us; the launch traced here: 91.1 us
  Pallas kernels  90.2 us (99%)
    pallas_call x1, Pallas kernels, comm(): pl.pallas_call(comm_kernel, out_shape=[pltpu.VMEM((8, PIECES, 128, 512),...  83.7 us
    pallas_call x1, Pallas kernels, write(): pl.pallas_call(write_kernel, out_shape=[jax.ShapeDtypeStruct(s, bf16) for...  6.44 us
  transfers between devices with their start and end apart: 1, of which 0 were waited for; matrix products, arithmetic and copies ran while one was open for 0% of the time, Pallas kernels for 7%

profile of v5, /device:TPU:1, one launch (start us, length us, event | category | flops | bytes accessed | tf_op | source)
XLA Modules:
  0.0 91.1 jit_solution(5415422515774152880)
XLA Ops:
  0.6 83.7 %comm.1 = (bf16[8,18,128,512]{3,2,1,0:T(8,128)(2,1)S(1)}, bf16[2,2,128,512]{3,2,1,0:T(8,128)(2,1)S(1)}, f32[2,4,8,128]{3,2,1,0:T(8,128)S(1)}) custom-call(bf16[1024,512]{1,0:T(8,128)(2,1)} %tq.1, bf16[64,1024]{1,0:T(8,128)(2,1)} %bitcast.11, bf16[64,1024]{1,0:T(8,128)(2,1)} %bitcast.12, bf16[512,1024]{1,0:T(8,128)(2,1)} %tm.1, bf16[16,1024]{1,0:T(8,128)(2,1)} %bitcast.13, ...), custom_call_target="tpu_custom_call" | custom-call | tf_op jit(solution)/shard_map/comm/pallas_call | solution.py:303
  84.3 0.2 collective-permute-start
  84.5 6.4 %write.1 = (bf16[4,128,8192]{2,1,0:T(8,128)(2,1)}, bf16[64,8192]{1,0:T(8,128)(2,1)}, bf16[64,8192]{1,0:T(8,128)(2,1)}, bf16[64,128,512]{2,1,0:T(8,128)(2,1)}, bf16[64,128]{1,0:T(8,128)(2,1)}) custom-call(bf16[8,18,128,512]{3,2,1,0:T(8,128)(2,1)S(1)} %get-tuple-element.15.b, bf16[2,2,128,512]{3,2,1,0:T(8,128)(2,1)S(1)} %get-tuple-element.16.late, ...), custom_call_target="tpu_custom_call" | custom-call | bytes 39845888 | tf_op jit(solution)/shard_map/write/pallas_call | solution.py:377
  91.0 0.0 collective-permute-done.other
  91.0 0.1 write_last.1
Async XLA Ops:
  84.3 6.7 %collective-permute-start = (bf16[2,2,128,512]{3,2,1,0:T(8,128)(2,1)S(1)}, bf16[2,2,128,512]{3,2,1,0:T(8,128)(2,1)S(1)}, u32[]{:S(2)}, u32[]{:S(2)}) collective-permute-start(bf16[2,2,128,512]{3,2,1,0:T(8,128)(2,1)S(1)} %get-tuple-element.16.late), channel_id=1, source_target_pairs={{0,16},{16,0},{32,48},{48,32},{64,80},{80,64},{96,112},{112,96},{1... | collective-permute-start | bytes 1572872 | tf_op jit(solution)/shard_map/ppermute | solution.py:424

commit v6 on v5

--- a/solution.py
+++ b/solution.py
@@ -54,7 +54,7 @@
         pl.semaphore_signal(barrier, inc=1, device_id=to_far, device_id_type=MESH)
 
     loads = [
-        (na, sna), (nb, snb), (tk, xk), (lk, slk), (hk, shk), (tv, xv), (lv, slv), (hv, shv),
+        (tk, xk), (lk, slk), (hk, shk), (na, sna), (nb, snb), (tv, xv), (lv, slv), (hv, shv),
         (lm, slm), (hm, shm), (tm, xm),
         (lq, slq), (hq, shq), (tq, xq),
     ]
@@ -337,13 +337,13 @@
 
 
 def write_kernel(b, late, nz, q, k, v, m, n, gain, sem):
-    tiles = [nz[r % 2, r // 2] for r in range(8)]
-    gain[...] = jnp.concatenate(tiles, axis=0).astype(jnp.bfloat16)
     for r in range(8):
         pltpu.make_async_copy(b.at[r, pl.ds(10, 8)], m.at[pl.ds(r * 8, 8)], sem.at[3]).start()
         for j in range(2):
             cols = pl.ds(r * 1024 + j * 512, 512)
             pltpu.make_async_copy(b.at[r, pl.ds(2 + 4 * j, 4)], q.at[:, :, cols], sem.at[2]).start()
+    tiles = [nz[r % 2, r // 2] for r in range(8)]
+    gain[...] = jnp.concatenate(tiles, axis=0).astype(jnp.bfloat16)
     rows = lax.axis_index("rows")
     core = rows % 2
     far = (rows // 2 + 2) % 4 * 2

time: 91.2 us -> 91.2 us (level)
  no operation moved by 1% of the time
where the time goes in v6:
time: 91.2 us; the launch traced here: 91 us
  Pallas kernels  90.2 us (99%)
    pallas_call x1, Pallas kernels, comm(): pl.pallas_call(comm_kernel, out_shape=[pltpu.VMEM((8, PIECES, 128, 512),...  83.7 us
    pallas_call x1, Pallas kernels, write(): pl.pallas_call(write_kernel, out_shape=[jax.ShapeDtypeStruct(s, bf16) for...  6.44 us
  transfers between devices with their start and end apart: 1, of which 0 were waited for; matrix products, arithmetic and copies ran while one was open for 0% of the time, Pallas kernels for 7%

profile of v6, /device:TPU:1, one launch (start us, length us, event | category | flops | bytes accessed | tf_op | source)
XLA Modules:
  0.0 91.0 jit_solution(6165625925434041996)
XLA Ops:
  0.6 83.7 %comm.1 = (bf16[8,18,128,512]{3,2,1,0:T(8,128)(2,1)S(1)}, bf16[2,2,128,512]{3,2,1,0:T(8,128)(2,1)S(1)}, f32[2,4,8,128]{3,2,1,0:T(8,128)S(1)}) custom-call(bf16[1024,512]{1,0:T(8,128)(2,1)} %tq.1, bf16[64,1024]{1,0:T(8,128)(2,1)} %bitcast.11, bf16[64,1024]{1,0:T(8,128)(2,1)} %bitcast.12, bf16[512,1024]{1,0:T(8,128)(2,1)} %tm.1, bf16[16,1024]{1,0:T(8,128)(2,1)} %bitcast.13, ...), custom_call_target="tpu_custom_call" | custom-call | tf_op jit(solution)/shard_map/comm/pallas_call | solution.py:303
  84.3 0.2 collective-permute-start
  84.5 6.4 %write.1 = (bf16[4,128,8192]{2,1,0:T(8,128)(2,1)}, bf16[64,8192]{1,0:T(8,128)(2,1)}, bf16[64,8192]{1,0:T(8,128)(2,1)}, bf16[64,128,512]{2,1,0:T(8,128)(2,1)}, bf16[64,128]{1,0:T(8,128)(2,1)}) custom-call(bf16[8,18,128,512]{3,2,1,0:T(8,128)(2,1)S(1)} %get-tuple-element.15.b, bf16[2,2,128,512]{3,2,1,0:T(8,128)(2,1)S(1)} %get-tuple-element.16.late, ...), custom_call_target="tpu_custom_call" | custom-call | bytes 39845888 | tf_op jit(solution)/shard_map/write/pallas_call | solution.py:377
  91.0 0.0 collective-permute-done.other
  91.0 0.1 write_last.1
Async XLA Ops:
  84.3 6.7 %collective-permute-start = (bf16[2,2,128,512]{3,2,1,0:T(8,128)(2,1)S(1)}, bf16[2,2,128,512]{3,2,1,0:T(8,128)(2,1)S(1)}, u32[]{:S(2)}, u32[]{:S(2)}) collective-permute-start(bf16[2,2,128,512]{3,2,1,0:T(8,128)(2,1)S(1)} %get-tuple-element.16.late), channel_id=1, source_target_pairs={{0,16},{16,0},{32,48},{48,32},{64,80},{80,64},{96,112},{112,96},{1... | collective-permute-start | bytes 1572872 | tf_op jit(solution)/shard_map/ppermute | solution.py:424
